TPU v7x, 8 devices: a whole 2x2x1 slice. The times are simulated.
8 devices in a mesh: dp: 2 (over z, y), sp: 4 (over x, core).
Axes of the slice: x: 2, y: 2, z: 1, core: 2. Of those that a mesh axis runs over, the one named last changes fastest.
Arguments:
- hidden: bfloat16 [24576, 896], P(('dp', 'sp')), parts along dimension 0
- tok_perm: int32 [24576], P(('dp', 'sp')), parts along dimension 0
- send_off: int32 [32], P(('dp', 'sp')), parts along dimension 0
- send_len: int32 [32], P(('dp', 'sp')), parts along dimension 0
- recv_off: int32 [32], P(('dp', 'sp')), parts along dimension 0
- recv_len: int32 [32], P(('dp', 'sp')), parts along dimension 0
- recv_doc: int32 [12288], P(('dp', 'sp')), parts along dimension 0
- recv_pos: int32 [12288], P(('dp', 'sp')), parts along dimension 0
- g_attn: bfloat16 [896], replicated
- w_q: bfloat16 [896, 14, 64], replicated
- w_k: bfloat16 [896, 2, 64], replicated
- w_v: bfloat16 [896, 2, 64], replicated
- w_o: bfloat16 [14, 64, 896], replicated
- g_mlp: bfloat16 [896], replicated
- w_gate: bfloat16 [896, 4864], replicated
- w_up: bfloat16 [896, 4864], replicated
- w_down: bfloat16 [4864, 896], replicated
Outputs:
- output: bfloat16 [24576, 896], P(('dp', 'sp')), parts along dimension 0
There are 2 independent parts. A program takes and returns all parts, laid end to end along the dimension named above; an argument that names none is the same for every part.
All inputs are finite; a program needn't handle non-finite values.
Results may differ from a plain program's by a relative error of at most 0.0108911.
Values are sent between devices in bfloat16 or wider.
A program may use at most 1 GiB of HBM per device.

v0:
```python
import functools

import jax
import jax.numpy as jnp
import numpy as np
from jax import lax
from jax.experimental import pallas as pl
from jax.experimental.pallas import tpu as pltpu
from jax.sharding import PartitionSpec as P

ROPE_BASE = 500000.0
NORM_EPS = 1e-5
ROWS = 512
QB = 256
FT = 256


def norm_rows(rows_f, gain):
    inv = lax.rsqrt(jnp.mean(rows_f * rows_f, axis=-1, keepdims=True) + NORM_EPS)
    return (rows_f * inv * gain).astype(jnp.bfloat16)


def rope_pair(x, cos_t, sin_t, first_half):
    swapped = jnp.where(first_half, pltpu.roll(x, 96, 1), pltpu.roll(x, 32, 1))
    return x * cos_t + swapped * sin_t


def dot_t(a, b):
    return lax.dot_general(a, b, (((1,), (1,)), ((), ())), preferred_element_type=jnp.float32)


def dot_n(a, b):
    return jnp.dot(a, b, preferred_element_type=jnp.float32)


def layer_kernel(span_ref, outgo, rloc_ref, pos_ref, freq_ref, ga_ref, gm_ref, wq_h, wk_h, wv_h, wo_h, wg_h, wu_h, wd_h, own, sib_out, far,
                 rbuf, r_s, q_s, k_s, v_s, o_s, m_s, obuf, sa, sb, bias, cos_s, sin_s, start_s, wq_s, wk_s, wv_s, wo_s, wg_s, wu_s, wd_s, sems,
                 as_, ar, ps, pr, ss, sr, fs, fr, own_sem):
    n_rows, dim = rloc_ref.shape
    n_pairs = dim // 128
    n_blk = n_rows // QB
    ff = wg_s.shape[1]
    me = lax.axis_index("sp")
    sib = me + 1 - 2 * lax.rem(me, 2)
    peer = lax.rem(me + 2, 4)
    loads = [pltpu.make_async_copy(a, b, sems.at[i]) for i, (a, b) in enumerate(
        [(wq_h, wq_s), (wk_h, wk_s), (wv_h, wv_s), (wo_h, wo_s), (wg_h, wg_s), (wu_h, wu_s), (wd_h, wd_s)])]
    meet([sib, peer])

    def rows_at(c):
        return pl.ds(pl.multiple_of(c * QB, QB), QB)

    def arrive(c):
        return push(outgo.at[rows_at(c)], rbuf.at[rows_at(c)], as_.at[c], ar.at[c], peer)

    def to_peer(c):
        return push(own.at[rows_at(c)], far.at[rows_at(c)], ps.at[c], pr.at[c], peer)

    def to_sib(c):
        return push(own.at[rows_at(c)], sib_out.at[rows_at(c)], ss.at[c], sr.at[c], sib)

    def forward(c):
        return push(far.at[rows_at(c)], far.at[pl.ds(pl.multiple_of(n_rows + c * QB, QB), QB)], fs.at[c], fr.at[c], sib)

    def keep(c):
        return pltpu.make_async_copy(obuf.at[lax.rem(c, 2)], own.at[rows_at(c)], own_sem.at[c])

    def send(c):
        keep(c).wait()
        to_peer(c).start()
        to_sib(c).start()

    def relay(c):
        to_peer(c).wait_recv()
        forward(c).start()

    for c in range(n_blk):
        arrive(c).start()
    for c in loads:
        c.start()
    gain_a = ga_ref[...].astype(jnp.float32).reshape(1, dim)
    gain_m = gm_ref[...].astype(jnp.float32).reshape(1, dim)
    first, last = span_ref[0], span_ref[1]
    tile_lane = lax.broadcasted_iota(jnp.int32, (128, 128), 1)
    tile_row = lax.broadcasted_iota(jnp.int32, (128, 128), 0)
    sign = jnp.where(tile_lane % 64 < 32, -1.0, 1.0)
    for t in range(n_rows // 128):
        rows = slice(128 * t, 128 * (t + 1))
        pos = jnp.transpose(jnp.broadcast_to(pos_ref[t:t + 1, :].astype(jnp.float32), (128, 128)))
        angle = pos * freq_ref[...]
        cos_s[rows, :] = jnp.cos(angle)
        sin_s[rows, :] = jnp.sin(angle) * sign
        start_s[rows, :] = 128 * t + tile_row - pos.astype(jnp.int32)
    for c in loads[:4]:
        c.wait()

    lane = lax.broadcasted_iota(jnp.int32, (QB, 128), 1)
    first_half = lane % 64 < 32
    low = lane < 64

    def attend(c):
        length = (c + 1) * QB
        start = start_s[c * QB:(c + 1) * QB, :]
        row = c * QB + lax.broadcasted_iota(jnp.int32, (QB, 128), 0)
        for t in range(length // 128):
            col = 128 * t + lane
            bias[:, 128 * t:128 * (t + 1)] = jnp.where((col >= start) & (col <= row), 3e38, -1e30)

        def scores(p, half, dst):
            qp = q_s[p]
            qh = jnp.where(low if half == 0 else ~low, qp, jnp.zeros_like(qp))
            s = jnp.minimum(dot_t(qh, k_s[(2 * p + half) // 7, :length, :]), bias[:, :length])
            dst[:, :length] = s
            return jnp.max(s, axis=1, keepdims=True)

        def soft(p, half, src, top):
            e = jnp.exp(src[:, :length] - top)
            total = jnp.sum(e, axis=1, keepdims=True)
            return dot_n(e.astype(jnp.bfloat16), v_s[(2 * p + half) // 7, :length, :]) / total

        def pair(p, top_a):
            top_b = scores(p, 1, sb)
            out_a = soft(p, 0, sa, top_a)
            top_a = scores(jnp.minimum(p + 1, n_pairs - 1), 0, sa)
            out_b = soft(p, 1, sb, top_b)
            o_s[:, pl.ds(pl.multiple_of(p * 128, 128), 128)] = jnp.where(low, out_a, out_b).astype(jnp.bfloat16)
            return top_a

        lax.fori_loop(0, n_pairs, pair, scores(0, 0, sa))

    @pl.loop(0, n_blk)
    def _block(c):
        rows = rows_at(c)
        arrive(c).wait_recv()
        where_row = c * QB + lax.broadcasted_iota(jnp.int32, (QB, dim), 0)
        arrived = (where_row >= first) & (where_row < last)
        r = jnp.where(arrived, rbuf[rows, :].astype(jnp.float32), rloc_ref[rows, :].astype(jnp.float32))
        r_s[...] = r
        h = norm_rows(r, gain_a)
        cos_t = cos_s[rows, :]
        sin_t = sin_s[rows, :]
        q = dot_t(h, wq_s[...])
        for p in range(n_pairs):
            qp = rope_pair(q[:, 128 * p:128 * (p + 1)], cos_t, sin_t, first_half)
            q_s[p] = (qp.astype(jnp.bfloat16) * 0.125).astype(jnp.bfloat16)
        k = rope_pair(dot_t(h, wk_s[...]), cos_t, sin_t, first_half)
        v = dot_t(h, wv_s[...])
        for s, x in ((k_s, k), (v_s, v)):
            other = pltpu.roll(x, 64, 1)
            s[0, rows, :] = jnp.where(low, x, other).astype(jnp.bfloat16)
            s[1, rows, :] = jnp.where(low, other, x).astype(jnp.bfloat16)

        for at in range(n_blk):
            pl.when(c == at)(functools.partial(attend, at))

        @pl.when(c >= 1)
        def _send():
            send(c - 1)

        @pl.when(c >= 4)
        def _relay():
            relay(c - 4)

        @pl.when(c == 0)
        def _weights():
            for x in loads[4:]:
                x.wait()

        attn = dot_n(o_s[...], wo_s[...]).astype(jnp.bfloat16)
        z = (r_s[...] + attn.astype(jnp.float32)).astype(jnp.bfloat16).astype(jnp.float32)
        r_s[...] = z
        h = norm_rows(z, gain_m)
        for t in range(ff // FT):
            cols = slice(t * FT, (t + 1) * FT)
            gate = 0.5 * dot_n(h, wg_s[:, cols])
            up = dot_n(h, wu_s[:, cols])
            m_s[:, cols] = ((gate + gate * jnp.tanh(gate)) * up).astype(jnp.bfloat16)
        down = dot_n(m_s[...], wd_s[...]).astype(jnp.bfloat16)
        obuf[lax.rem(c, 2)] = (r_s[...] + down.astype(jnp.float32)).astype(jnp.bfloat16)
        keep(c).start()

    send(n_blk - 1)
    for c in range(n_blk - 4, n_blk):
        relay(c)
    for c in range(n_blk):
        arrive(c).wait_send()
        to_sib(c).wait()
        to_peer(c).wait_send()
        forward(c).wait()


def layer(span, outgo, rloc, positions, g_attn, w_q, w_k, w_v, w_o, g_mlp, w_gate, w_up, w_down):
    n_rows, dim = rloc.shape
    head_dim = w_q.shape[2]
    half_dim = head_dim // 2
    exponent = -2.0 * np.arange(half_dim, dtype=np.float32) / np.float32(head_dim)
    inv_freq = np.power(np.float32(ROPE_BASE), exponent).astype(np.float32)
    freq = jnp.asarray(np.tile(inv_freq, 128 // half_dim)[None, :])
    wq_t = jnp.transpose(w_q, (1, 2, 0)).reshape(dim, dim)
    wk_t = jnp.transpose(w_k, (1, 2, 0)).reshape(128, dim)
    wv_t = jnp.transpose(w_v, (1, 2, 0)).reshape(128, dim)
    wo_t = w_o.reshape(dim, dim)
    bf, f32 = jnp.bfloat16, jnp.float32
    n_blk = n_rows // QB
    ff = w_gate.shape[1]
    rows = jax.ShapeDtypeStruct((n_rows, dim), bf)
    dma = pltpu.SemaphoreType.DMA
    return pl.pallas_call(
        layer_kernel,
        out_shape=[rows, rows, jax.ShapeDtypeStruct((2 * n_rows, dim), bf)],
        in_specs=[SM, ANY] + [VM] * 5 + [ANY] * 7,
        out_specs=[ANY] * 3,
        scratch_shapes=[
            pltpu.VMEM((n_rows, dim), bf), pltpu.VMEM((QB, dim), f32), pltpu.VMEM((dim // 128, QB, 128), bf),
            pltpu.VMEM((2, n_rows, 128), bf), pltpu.VMEM((2, n_rows, 128), bf), pltpu.VMEM((QB, dim), bf),
            pltpu.VMEM((QB, ff), bf), pltpu.VMEM((2, QB, dim), bf)]
            + [pltpu.VMEM((QB, n_rows), f32)] * 3
            + [pltpu.VMEM((n_rows, 128), f32), pltpu.VMEM((n_rows, 128), f32), pltpu.VMEM((n_rows, 128), jnp.int32),
               pltpu.VMEM((dim, dim), bf), pltpu.VMEM((128, dim), bf), pltpu.VMEM((128, dim), bf), pltpu.VMEM((dim, dim), bf),
               pltpu.VMEM((dim, ff), bf), pltpu.VMEM((dim, ff), bf), pltpu.VMEM((ff, dim), bf), dma((7,))] + [dma((n_blk,))] * 9,
        compiler_params=pltpu.CompilerParams(collective_id=1, has_side_effects=True, vmem_limit_bytes=67000000),
        name="layer",
    )(span, outgo, rloc, positions.reshape(-1, 128), freq, g_attn, g_mlp, wq_t, wk_t, wv_t, wo_t, w_gate, w_up, w_down)


CHUNK = 128
MESH_ID = pl.DeviceIdType.MESH
ANY = pl.BlockSpec(memory_space=pl.ANY)
VM = pl.BlockSpec(memory_space=pltpu.VMEM)
SM = pl.BlockSpec(memory_space=pltpu.SMEM)


def meet(devices):
    barrier = pltpu.get_barrier_semaphore()
    for dev in devices:
        pl.semaphore_signal(barrier, inc=1, device_id={"sp": dev}, device_id_type=MESH_ID)
    pl.semaphore_wait(barrier, len(devices))


def push(src, dst, send_sem, recv_sem, dev):
    return pltpu.make_async_remote_copy(src_ref=src, dst_ref=dst, send_sem=send_sem, recv_sem=recv_sem,
                                        device_id={"sp": dev}, device_id_type=MESH_ID)


def share_kernel(n_split, *refs):
    n = (len(refs) - 2) // 2
    ins, outs, send_sems, recv_sems = refs[:n], refs[n:2 * n], refs[-2], refs[-1]
    me = lax.axis_index("sp")
    sib = me + 1 - 2 * lax.rem(me, 2)
    meet([sib])
    copies = []
    for a, b in zip(ins, outs):
        parts = n_split if a.ndim == 2 else 1
        step = a.shape[0] // parts
        for p in range(parts):
            rows = pl.ds(p * step, step)
            copies.append((a.at[rows], b.at[rows]) if parts > 1 else (a, b))
    started = []
    for i, (a, b) in enumerate(copies):
        cp = push(a, b, send_sems.at[i], recv_sems.at[i], sib)
        cp.start()
        started.append(cp)
    for cp in started:
        cp.wait()


def share(arrays, collective_id):
    return pl.pallas_call(
        functools.partial(share_kernel, 4),
        out_shape=[jax.ShapeDtypeStruct(a.shape, a.dtype) for a in arrays],
        in_specs=[ANY] * len(arrays), out_specs=[ANY] * len(arrays),
        scratch_shapes=[pltpu.SemaphoreType.DMA((16,)), pltpu.SemaphoreType.DMA((16,))],
        compiler_params=pltpu.CompilerParams(collective_id=collective_id, has_side_effects=True),
        name="share",
    )(*arrays)


LOAD = 512


def load_table(parts, tab, stage, sems):
    jobs = []
    for ref, blocks in parts:
        for i in range(ref.shape[0] // LOAD):
            n = len(jobs)
            copy = pltpu.make_async_copy(ref.at[pl.ds(i * LOAD, LOAD)], stage.at[pl.ds(n * LOAD, LOAD)], sems.at[n])
            jobs.append((copy, None if blocks is None else i < blocks))
    for copy, cond in jobs:
        if cond is None:
            copy.start()
        else:
            pl.when(cond)(copy.start)
    for n, (copy, cond) in enumerate(jobs):
        def fill(n=n, copy=copy):
            copy.wait()
            fill_table(stage, n * LOAD, tab, n * LOAD)
        if cond is None:
            fill()
        else:
            pl.when(cond)(fill)


def fill_table(stage, at, tab, base):
    @pl.loop(0, LOAD // 64)
    def _blk(i):
        rows = pl.ds(pl.multiple_of(at + i * 64, 64), 64)
        first = pl.multiple_of((base + i * 64) * 8, 8)
        for j in range(stage.shape[1] // 128):
            tab[pl.ds(first + j, 64, stride=8), :] = stage[rows, 128 * j:128 * (j + 1)].astype(jnp.float32)


UNROLL = 16


def slab(k):
    return pl.ds(pl.multiple_of(k * 8, 8), 8)


def copy_rows(n_rows, move):
    @pl.loop(0, n_rows // UNROLL)
    def _grp(i):
        for k in range(UNROLL):
            move(i * UNROLL + k)


def rows_out(n_rows, src3, dst):
    @pl.loop(0, n_rows // CHUNK)
    def _blk(i):
        rows = pl.ds(pl.multiple_of(i * CHUNK, CHUNK), CHUNK)
        for j in range(dst.shape[1] // 128):
            dst[rows, 128 * j:128 * (j + 1)] = src3[pl.ds(pl.multiple_of(i * CHUNK * 8, 8) + j, CHUNK, stride=8), :].astype(dst.dtype)


def move_run(n, one):
    whole = n // UNROLL

    @pl.loop(0, whole)
    def _grp(i):
        for k in range(UNROLL):
            one(i * UNROLL + k)

    @pl.loop(whole * UNROLL, n)
    def _one(i):
        one(i)


def pick_kernel(perm, so, sl, ro, rl, perm_b, so_b, sl_b, ro_b, rl_b, own, sib, outgo, rloc, span, tab, out3, stage, sems):
    cap = rloc.shape[0]
    n_tok = own.shape[0]
    me = lax.axis_index("sp")
    core = lax.rem(me, 2)
    chip = me // 2
    mate = me + 1 - 2 * core
    near, far = 2 * chip, 2 * (1 - chip)
    load_table([(own, None), (sib, None)], tab, stage, sems)
    n_in = rl[far] + rl[far + 1]
    span[0] = (1 - chip) * (cap - n_in)
    span[1] = (1 - chip) * (cap - n_in) + n_in

    def run(dst_row, src, table_row, at, n):
        def one(t):
            out3[slab(dst_row + t), :] = tab[slab(table_row + src[at + t]), :]
        move_run(n, one)

    goal = far + core
    row = chip * (cap - sl[goal] - sl_b[goal])
    run(row + core * sl_b[goal], perm, 0, so[goal], sl[goal])
    run(row + (1 - core) * sl[goal], perm_b, n_tok, so_b[goal], sl_b[goal])
    rows_out(cap, out3, outgo)
    run(ro[me], perm, 0, so[me], sl[me])
    run(ro[mate], perm_b, n_tok, so_b[me], sl_b[me])
    rows_out(cap, out3, rloc)


def back_place_kernel(perm, so, sl, ro, rl, perm_b, so_b, sl_b, ro_b, rl_b, own, sib, stream, out, tab, out3, stage, sems):
    cap = own.shape[0]
    n_tok = out.shape[0]
    me = lax.axis_index("sp")
    core = lax.rem(me, 2)
    chip = me // 2
    mate = me + 1 - 2 * core
    far = 2 * (1 - chip)
    load_table([(own, None), (sib, None), (stream, None)], tab, stage, sems)

    def run(goal, row):
        def one(t):
            out3[slab(perm[so[goal] + t]), :] = tab[slab(row + t), :]
        move_run(sl[goal], one)

    run(me, ro[me])
    run(mate, cap + ro_b[me])
    for goal, base in ((far + core, 2 * cap), (far + 1 - core, 3 * cap)):
        run(goal, base + chip * (cap - sl[goal] - sl_b[goal]) + core * sl_b[goal])
    sent = so[3] + sl[3]

    def blank(t):
        out3[slab(perm[sent + t]), :] = jnp.zeros((8, 128), jnp.float32)

    move_run(n_tok - sent, blank)
    rows_out(n_tok, out3, out)


def local_call(body, out_shapes, out_specs, n_any, tab_rows, out_rows, dim, name):
    return pl.pallas_call(
        body,
        out_shape=out_shapes,
        in_specs=[SM] * 10 + [ANY] * n_any,
        out_specs=out_specs,
        scratch_shapes=[pltpu.VMEM((tab_rows * 8, 128), jnp.float32), pltpu.VMEM((out_rows * 8, 128), jnp.float32),
                        pltpu.VMEM((tab_rows, dim), jnp.bfloat16), pltpu.SemaphoreType.DMA((tab_rows // LOAD,))],
        compiler_params=pltpu.CompilerParams(vmem_limit_bytes=66000000),
        name=name,
    )


def solution(mesh):
    row_spec = P(('dp', 'sp'), None)
    vec_spec = P(('dp', 'sp'))
    rep_spec = P()

    def per_device(hidden, tok_perm, send_off, send_len, recv_off, recv_len, recv_doc, recv_pos, g_attn, w_q, w_k, w_v, w_o, g_mlp, w_gate, w_up, w_down):
        n_tok, dim = hidden.shape
        cap = recv_doc.shape[0]
        plan = [tok_perm, send_off, send_len, recv_off, recv_len]
        sib_hidden, *sib_plan = share([hidden] + plan, 0)
        rows_bf = jax.ShapeDtypeStruct((cap, dim), hidden.dtype)
        outs = [rows_bf, rows_bf, jax.ShapeDtypeStruct((2,), jnp.int32)]
        outgo, rloc, span = local_call(pick_kernel, outs, [VM, VM, SM], 2, 2 * n_tok, cap, dim, "pick")(*plan, *sib_plan, hidden, sib_hidden)
        done, sib_done, returned = layer(span, outgo, rloc, recv_pos, g_attn, w_q, w_k, w_v, w_o, g_mlp, w_gate, w_up, w_down)
        out = jax.ShapeDtypeStruct((n_tok, dim), hidden.dtype)
        return local_call(back_place_kernel, out, VM, 3, 4 * cap, n_tok, dim, "back_place")(*plan, *sib_plan, done, sib_done, returned)

    return jax.shard_map(per_device, mesh=mesh, in_specs=(row_spec,) + (vec_spec,) * 7 + (rep_spec,) * 9, out_specs=row_spec, check_vma=False)
```

profile of v0, /device:TPU:0, one launch (start us, length us, event | category | flops | bytes accessed | tf_op | source)
XLA Modules:
  0.0 168.0 jit_solution(2962206335125202437)
XLA Ops:
  0.0 9.8 %share.1 = (bf16[3072,896]{1,0:T(8,128)(2,1)}, s32[3072]{0:T(1024)}, s32[4]{0:T(128)}, s32[4]{0:T(128)}, s32[4]{0:T(128)}, /*index=5*/s32[4]{0:T(128)}) custom-call(bf16[3072,896]{1,0:T(8,128)(2,1)} %own.1, s32[3072]{0:T(1024)} %perm.3, s32[4]{0:T(128)} %so.3, s32[4]{0:T(128)} %sl.3, s32[4]{0:T(128)} %ro.3, s32[4]{0:T(128)} %rl.3), custom_call_target="tpu_custom_call" | custom-call | tf_op jit(solution)/shard_map/share/pallas_call | solution.py:268
  9.8 14.8 %pick.1 = (bf16[1536,896]{1,0:T(8,128)(2,1)}, bf16[1536,896]{1,0:T(8,128)(2,1)}, s32[2]{0:T(128)}) custom-call(s32[3072]{0:T(1024)} %perm.3, s32[4]{0:T(128)} %so.3, s32[4]{0:T(128)} %sl.3, s32[4]{0:T(128)} %ro.3, s32[4]{0:T(128)} %rl.3, s32[3072]{0:T(1024)} %get-tuple-element.17.perm_b, s32[4]{0:T(128)} %get-tuple-element.18.so_b, ...), custom_call_target="tpu_custom_call" | custom-call | tf_op jit(solution)/shard_map/pick/pallas_call | solution.py:428
  24.6 125.9 %layer.1 = (bf16[1536,896]{1,0:T(8,128)(2,1)}, bf16[1536,896]{1,0:T(8,128)(2,1)}, bf16[3072,896]{1,0:T(8,128)(2,1)}) custom-call(s32[2]{0:T(128)} %get-tuple-element.23.span_ref, bf16[1536,896]{1,0:T(8,128)(2,1)} %get-tuple-element.24.outgo, bf16[1536,896]{1,0:T(8,128)(2,1)} %get-tuple-element.25.rloc_ref, s32[12,128]{1,0:T(8,128)} %bitcast.15, ...), custom_call_target="tpu_custom_call" | custom-call | tf_op jit(solution)/shard_map/layer/pallas_call | solution.py:208
  150.5 17.3 %back_place.1 = bf16[3072,896]{1,0:T(8,128)(2,1)} custom-call(s32[3072]{0:T(1024)} %perm.3, s32[4]{0:T(128)} %so.3, s32[4]{0:T(128)} %sl.3, s32[4]{0:T(128)} %ro.3, s32[4]{0:T(128)} %rl.3, s32[3072]{0:T(1024)} %get-tuple-element.17.perm_b, s32[4]{0:T(128)} %get-tuple-element.18.so_b, s32[4]{0:T(128)} %get-tuple-element.19.sl_b, s32[4]{0:T(128)} %get-tuple-element.20.ro_b, ...), custom_call_target="tpu_custom_call" | custom-call | tf_op jit(solution)/shard_map/back_place/pallas_call | solution.py:431
where the time goes:
time: 171 us; the launch traced here: 168 us
  Pallas kernels  168 us (98%)
    pallas_call x1, Pallas kernels, layer(): pl.pallas_call(layer_kernel, out_shape=[rows, rows, jax.ShapeDtypeStruct(...  126 us
    pallas_call x1, Pallas kernels, per_device(): local_call(back_place_kernel, out, VM, 3, 4 * cap, n_tok, dim, 'back_place')  17.3 us
    pallas_call x1, Pallas kernels, per_device(): local_call(pick_kernel, outs, [VM, VM, SM], 2, 2 * n_tok, cap, dim, 'pick')  14.8 us
    pallas_call x1, Pallas kernels, share(): pl.pallas_call(functools.partial(share_kernel, 4), out_shape=[jax.ShapeDt...  9.84 us

commit v1 on v0

--- a/solution.py
+++ b/solution.py
@@ -276,39 +276,42 @@
 
 
 LOAD = 512
+FILL = 64
+PITCH = 9
 
 
 def load_table(parts, tab, stage, sems):
     jobs = []
-    for ref, blocks in parts:
+    for ref, lo, hi in parts:
         for i in range(ref.shape[0] // LOAD):
             n = len(jobs)
             copy = pltpu.make_async_copy(ref.at[pl.ds(i * LOAD, LOAD)], stage.at[pl.ds(n * LOAD, LOAD)], sems.at[n])
-            jobs.append((copy, None if blocks is None else i < blocks))
-    for copy, cond in jobs:
+            if lo is None:
+                jobs.append((copy, None, 0, LOAD // FILL))
+            else:
+                low, high = jnp.maximum(lo - i * LOAD, 0), jnp.minimum(hi - i * LOAD, LOAD)
+                jobs.append((copy, low < high, low // FILL, (high + FILL - 1) // FILL))
+    for copy, cond, _, _ in jobs:
         if cond is None:
             copy.start()
         else:
             pl.when(cond)(copy.start)
-    for n, (copy, cond) in enumerate(jobs):
-        def fill(n=n, copy=copy):
+    for n, (copy, cond, low, high) in enumerate(jobs):
+        def fill(n=n, copy=copy, low=low, high=high):
             copy.wait()
-            fill_table(stage, n * LOAD, tab, n * LOAD)
+
+            @pl.loop(low, high)
+            def _blk(i):
+                rows = pl.ds(pl.multiple_of(n * LOAD + i * FILL, FILL), FILL)
+                first = (n * LOAD + i * FILL) * PITCH
+                for j in range(stage.shape[1] // 128):
+                    tab[pl.ds(first + j, FILL, stride=PITCH), :] = stage[rows, 128 * j:128 * (j + 1)].astype(jnp.float32)
         if cond is None:
             fill()
         else:
             pl.when(cond)(fill)
 
 
-def fill_table(stage, at, tab, base):
-    @pl.loop(0, LOAD // 64)
-    def _blk(i):
-        rows = pl.ds(pl.multiple_of(at + i * 64, 64), 64)
-        first = pl.multiple_of((base + i * 64) * 8, 8)
-        for j in range(stage.shape[1] // 128):
-            tab[pl.ds(first + j, 64, stride=8), :] = stage[rows, 128 * j:128 * (j + 1)].astype(jnp.float32)
-
-
 UNROLL = 16
 
 
@@ -316,19 +319,28 @@
     return pl.ds(pl.multiple_of(k * 8, 8), 8)
 
 
-def copy_rows(n_rows, move):
-    @pl.loop(0, n_rows // UNROLL)
-    def _grp(i):
-        for k in range(UNROLL):
-            move(i * UNROLL + k)
-
-
-def rows_out(n_rows, src3, dst):
-    @pl.loop(0, n_rows // CHUNK)
+def rows_out(lo, hi, src3, stage, base, dst, sem):
+    first, last = lo // CHUNK, (hi + CHUNK - 1) // CHUNK
+
+    def copy(i):
+        rows = pl.multiple_of(i * CHUNK, CHUNK)
+        return pltpu.make_async_copy(stage.at[pl.ds(base + rows, CHUNK)], dst.at[pl.ds(rows, CHUNK)], sem)
+
+    @pl.loop(first, last)
     def _blk(i):
-        rows = pl.ds(pl.multiple_of(i * CHUNK, CHUNK), CHUNK)
+        rows = pl.ds(pl.multiple_of(base + i * CHUNK, CHUNK), CHUNK)
         for j in range(dst.shape[1] // 128):
-            dst[rows, 128 * j:128 * (j + 1)] = src3[pl.ds(pl.multiple_of(i * CHUNK * 8, 8) + j, CHUNK, stride=8), :].astype(dst.dtype)
+            stage[rows, 128 * j:128 * (j + 1)] = src3[pl.ds(i * CHUNK * PITCH + j, CHUNK, stride=PITCH), :].astype(stage.dtype)
+        copy(i).start()
+
+    def finish():
+        pl.loop(first, last)(lambda i: copy(i).wait())
+
+    return finish
+
+
+def slab(k):
+    return pl.ds(k * PITCH, 8)
 
 
 def move_run(n, one):
@@ -344,15 +356,15 @@
         one(i)
 
 
-def pick_kernel(perm, so, sl, ro, rl, perm_b, so_b, sl_b, ro_b, rl_b, own, sib, outgo, rloc, span, tab, out3, stage, sems):
+def pick_kernel(perm, so, sl, ro, rl, perm_b, so_b, sl_b, ro_b, rl_b, own, sib, outgo, rloc, span, tab, out3, stage, sems, out_sems):
     cap = rloc.shape[0]
     n_tok = own.shape[0]
     me = lax.axis_index("sp")
     core = lax.rem(me, 2)
     chip = me // 2
     mate = me + 1 - 2 * core
-    near, far = 2 * chip, 2 * (1 - chip)
-    load_table([(own, None), (sib, None)], tab, stage, sems)
+    far = 2 * (1 - chip)
+    load_table([(own, None, None), (sib, None, None)], tab, stage, sems)
     n_in = rl[far] + rl[far + 1]
     span[0] = (1 - chip) * (cap - n_in)
     span[1] = (1 - chip) * (cap - n_in) + n_in
@@ -363,16 +375,20 @@
         move_run(n, one)
 
     goal = far + core
-    row = chip * (cap - sl[goal] - sl_b[goal])
+    n_out = sl[goal] + sl_b[goal]
+    row = chip * (cap - n_out)
     run(row + core * sl_b[goal], perm, 0, so[goal], sl[goal])
     run(row + (1 - core) * sl[goal], perm_b, n_tok, so_b[goal], sl_b[goal])
-    rows_out(cap, out3, outgo)
+    finish_out = rows_out(row, row + n_out, out3, stage, 0, outgo, out_sems.at[0])
+    near = chip * n_in
     run(ro[me], perm, 0, so[me], sl[me])
     run(ro[mate], perm_b, n_tok, so_b[me], sl_b[me])
-    rows_out(cap, out3, rloc)
-
-
-def back_place_kernel(perm, so, sl, ro, rl, perm_b, so_b, sl_b, ro_b, rl_b, own, sib, stream, out, tab, out3, stage, sems):
+    finish_loc = rows_out(near, near + cap - n_in, out3, stage, cap, rloc, out_sems.at[1])
+    finish_out()
+    finish_loc()
+
+
+def back_place_kernel(perm, so, sl, ro, rl, perm_b, so_b, sl_b, ro_b, rl_b, own, sib, stream, out, tab, out3, stage, sems, out_sems):
     cap = own.shape[0]
     n_tok = out.shape[0]
     me = lax.axis_index("sp")
@@ -380,24 +396,24 @@
     chip = me // 2
     mate = me + 1 - 2 * core
     far = 2 * (1 - chip)
-    load_table([(own, None), (sib, None), (stream, None)], tab, stage, sems)
-
-    def run(goal, row):
-        def one(t):
+
+    def far_row(goal):
+        return chip * (cap - sl[goal] - sl_b[goal]) + core * sl_b[goal]
+
+    runs = [(me, own, ro[me]), (mate, sib, ro_b[me]),
+            (far + core, stream.at[pl.ds(0, cap)], far_row(far + core)), (far + 1 - core, stream.at[pl.ds(cap, cap)], far_row(far + 1 - core))]
+    load_table([(ref, row, row + sl[goal]) for goal, ref, row in runs], tab, stage, sems)
+    for n, (goal, _, row) in enumerate(runs):
+        def one(t, goal=goal, row=n * cap + row):
             out3[slab(perm[so[goal] + t]), :] = tab[slab(row + t), :]
         move_run(sl[goal], one)
-
-    run(me, ro[me])
-    run(mate, cap + ro_b[me])
-    for goal, base in ((far + core, 2 * cap), (far + 1 - core, 3 * cap)):
-        run(goal, base + chip * (cap - sl[goal] - sl_b[goal]) + core * sl_b[goal])
     sent = so[3] + sl[3]
 
     def blank(t):
         out3[slab(perm[sent + t]), :] = jnp.zeros((8, 128), jnp.float32)
 
     move_run(n_tok - sent, blank)
-    rows_out(n_tok, out3, out)
+    rows_out(0, n_tok, out3, stage, 0, out, out_sems.at[0])()
 
 
 def local_call(body, out_shapes, out_specs, n_any, tab_rows, out_rows, dim, name):
@@ -406,8 +422,8 @@
         out_shape=out_shapes,
         in_specs=[SM] * 10 + [ANY] * n_any,
         out_specs=out_specs,
-        scratch_shapes=[pltpu.VMEM((tab_rows * 8, 128), jnp.float32), pltpu.VMEM((out_rows * 8, 128), jnp.float32),
-                        pltpu.VMEM((tab_rows, dim), jnp.bfloat16), pltpu.SemaphoreType.DMA((tab_rows // LOAD,))],
+        scratch_shapes=[pltpu.VMEM((tab_rows * PITCH, 128), jnp.float32), pltpu.VMEM((out_rows * PITCH, 128), jnp.float32),
+                        pltpu.VMEM((tab_rows, dim), jnp.bfloat16), pltpu.SemaphoreType.DMA((tab_rows // LOAD,)), pltpu.SemaphoreType.DMA((2,))],
         compiler_params=pltpu.CompilerParams(vmem_limit_bytes=66000000),
         name=name,
     )
@@ -425,9 +441,9 @@
         sib_hidden, *sib_plan = share([hidden] + plan, 0)
         rows_bf = jax.ShapeDtypeStruct((cap, dim), hidden.dtype)
         outs = [rows_bf, rows_bf, jax.ShapeDtypeStruct((2,), jnp.int32)]
-        outgo, rloc, span = local_call(pick_kernel, outs, [VM, VM, SM], 2, 2 * n_tok, cap, dim, "pick")(*plan, *sib_plan, hidden, sib_hidden)
+        outgo, rloc, span = local_call(pick_kernel, outs, [ANY, ANY, SM], 2, 2 * n_tok, cap, dim, "pick")(*plan, *sib_plan, hidden, sib_hidden)
         done, sib_done, returned = layer(span, outgo, rloc, recv_pos, g_attn, w_q, w_k, w_v, w_o, g_mlp, w_gate, w_up, w_down)
         out = jax.ShapeDtypeStruct((n_tok, dim), hidden.dtype)
-        return local_call(back_place_kernel, out, VM, 3, 4 * cap, n_tok, dim, "back_place")(*plan, *sib_plan, done, sib_done, returned)
+        return local_call(back_place_kernel, out, ANY, 3, 4 * cap, n_tok, dim, "back_place")(*plan, *sib_plan, done, sib_done, returned)
 
     return jax.shard_map(per_device, mesh=mesh, in_specs=(row_spec,) + (vec_spec,) * 7 + (rep_spec,) * 9, out_specs=row_spec, check_vma=False)

time: 171 us -> 162 us (0.947)
  Pallas kernels: 168 us -> 159 us
    pallas_call x2, Pallas kernels: 32 us -> 21.9 us  [the longest x1 11.5 us: per_device(): local_call(back_place_kernel, out, ANY, 3, 4 * cap, n_tok, dim, 'back_pla...]
    pallas_call x1, Pallas kernels: 126 us -> 128 us  [layer(): pl.pallas_call(layer_kernel, out_shape=[rows, rows, jax.ShapeDtypeStruct(...]
where the time goes in v1:
time: 162 us; the launch traced here: 160 us
  Pallas kernels  159 us (98%)
    pallas_call x1, Pallas kernels, layer(): pl.pallas_call(layer_kernel, out_shape=[rows, rows, jax.ShapeDtypeStruct(...  128 us
    pallas_call x1, Pallas kernels, per_device(): local_call(back_place_kernel, out, ANY, 3, 4 * cap, n_tok, dim, 'back_pla...  11.5 us
    pallas_call x1, Pallas kernels, per_device(): local_call(pick_kernel, outs, [ANY, ANY, SM], 2, 2 * n_tok, cap, dim, 'pi...  10.4 us
    pallas_call x1, Pallas kernels, share(): pl.pallas_call(functools.partial(share_kernel, 4), out_shape=[jax.ShapeDt...  9.84 us

profile of v1, /device:TPU:0, one launch (start us, length us, event | category | flops | bytes accessed | tf_op | source)
XLA Modules:
  0.0 159.6 jit_solution(6443433737415315195)
XLA Ops:
  0.0 9.8 %share.1 = (bf16[3072,896]{1,0:T(8,128)(2,1)}, s32[3072]{0:T(1024)}, s32[4]{0:T(128)}, s32[4]{0:T(128)}, s32[4]{0:T(128)}, /*index=5*/s32[4]{0:T(128)}) custom-call(bf16[3072,896]{1,0:T(8,128)(2,1)} %own.1, s32[3072]{0:T(1024)} %perm.3, s32[4]{0:T(128)} %so.3, s32[4]{0:T(128)} %sl.3, s32[4]{0:T(128)} %ro.3, s32[4]{0:T(128)} %rl.3), custom_call_target="tpu_custom_call" | custom-call | tf_op jit(solution)/shard_map/share/pallas_call | solution.py:268
  9.8 10.4 %pick.1 = (bf16[1536,896]{1,0:T(8,128)(2,1)}, bf16[1536,896]{1,0:T(8,128)(2,1)}, s32[2]{0:T(128)}) custom-call(s32[3072]{0:T(1024)} %perm.3, s32[4]{0:T(128)} %so.3, s32[4]{0:T(128)} %sl.3, s32[4]{0:T(128)} %ro.3, s32[4]{0:T(128)} %rl.3, s32[3072]{0:T(1024)} %get-tuple-element.17.perm_b, s32[4]{0:T(128)} %get-tuple-element.18.so_b, ...), custom_call_target="tpu_custom_call" | custom-call | tf_op jit(solution)/shard_map/pick/pallas_call | solution.py:444
  20.3 127.7 %layer.1 = (bf16[1536,896]{1,0:T(8,128)(2,1)}, bf16[1536,896]{1,0:T(8,128)(2,1)}, bf16[3072,896]{1,0:T(8,128)(2,1)}) custom-call(s32[2]{0:T(128)} %get-tuple-element.23.span_ref, bf16[1536,896]{1,0:T(8,128)(2,1)} %get-tuple-element.24.outgo, bf16[1536,896]{1,0:T(8,128)(2,1)} %get-tuple-element.25.rloc_ref, s32[12,128]{1,0:T(8,128)} %bitcast.15, ...), custom_call_target="tpu_custom_call" | custom-call | tf_op jit(solution)/shard_map/layer/pallas_call | solution.py:208
  148.0 11.5 %back_place.1 = bf16[3072,896]{1,0:T(8,128)(2,1)} custom-call(s32[3072]{0:T(1024)} %perm.3, s32[4]{0:T(128)} %so.3, s32[4]{0:T(128)} %sl.3, s32[4]{0:T(128)} %ro.3, s32[4]{0:T(128)} %rl.3, s32[3072]{0:T(1024)} %get-tuple-element.17.perm_b, s32[4]{0:T(128)} %get-tuple-element.18.so_b, s32[4]{0:T(128)} %get-tuple-element.19.sl_b, s32[4]{0:T(128)} %get-tuple-element.20.ro_b, ...), custom_call_target="tpu_custom_call" | custom-call | tf_op jit(solution)/shard_map/back_place/pallas_call | solution.py:447

commit v2 on v1

--- a/solution.py
+++ b/solution.py
@@ -33,10 +33,10 @@
     return jnp.dot(a, b, preferred_element_type=jnp.float32)
 
 
-def layer_kernel(span_ref, outgo, rloc_ref, pos_ref, freq_ref, ga_ref, gm_ref, wq_h, wk_h, wv_h, wo_h, wg_h, wu_h, wd_h, own, sib_out, far,
-                 rbuf, r_s, q_s, k_s, v_s, o_s, m_s, obuf, sa, sb, bias, cos_s, sin_s, start_s, wq_s, wk_s, wv_s, wo_s, wg_s, wu_s, wd_s, sems,
-                 as_, ar, ps, pr, ss, sr, fs, fr, own_sem):
-    n_rows, dim = rloc_ref.shape
+def layer_kernel(span_ref, out_a, out_b, loc_a, loc_b, pos_ref, freq_ref, ga_ref, gm_ref, wq_h, wk_h, wv_h, wo_h, wg_h, wu_h, wd_h, own, sib_out, far,
+                 rbuf, oa, ob, la, lb, r_s, q_s, k_s, v_s, o_s, m_s, obuf, sa, sb, bias, cos_s, sin_s, start_s, wq_s, wk_s, wv_s, wo_s, wg_s, wu_s, wd_s, sems,
+                 as_, ar, ps, pr, ss, sr, fs, fr, own_sem, oas, obs, obr, las, lbs, lbr):
+    n_rows, dim = loc_a.shape
     n_pairs = dim // 128
     n_blk = n_rows // QB
     ff = wg_s.shape[1]
@@ -51,7 +51,7 @@
         return pl.ds(pl.multiple_of(c * QB, QB), QB)
 
     def arrive(c):
-        return push(outgo.at[rows_at(c)], rbuf.at[rows_at(c)], as_.at[c], ar.at[c], peer)
+        return push(ob.at[rows_at(c)], rbuf.at[rows_at(c)], as_.at[c], ar.at[c], peer)
 
     def to_peer(c):
         return push(own.at[rows_at(c)], far.at[rows_at(c)], ps.at[c], pr.at[c], peer)
@@ -74,10 +74,31 @@
         to_peer(c).wait_recv()
         forward(c).start()
 
+    def fetch(c, src, dst, sem):
+        return pltpu.make_async_copy(src.at[rows_at(c)], dst.at[rows_at(c)], sem.at[c])
+
+    def trade(c, src, dst, send_sem, recv_sem):
+        return push(src.at[rows_at(c)], dst.at[rows_at(c)], send_sem.at[c], recv_sem.at[c], sib)
+
+    def select(c, lo, hi, yes, no):
+        row = c * QB + lax.broadcasted_iota(jnp.int32, (QB, dim), 0)
+        return jnp.where((row >= lo) & (row < hi), yes.astype(jnp.float32), no.astype(jnp.float32))
+
     for c in range(n_blk):
-        arrive(c).start()
+        trade(c, out_b, ob, obs, obr).start()
+        fetch(c, out_a, oa, oas).start()
+    for c in range(n_blk):
+        trade(c, loc_b, lb, lbs, lbr).start()
+        fetch(c, loc_a, la, las).start()
     for c in loads:
         c.start()
+    for c in range(n_blk):
+        trade(c, out_b, ob, obs, obr).wait_recv()
+        fetch(c, out_a, oa, oas).wait()
+        rows = rows_at(c)
+        ob[rows, :] = select(c, span_ref[2], span_ref[3], oa[rows, :], ob[rows, :]).astype(jnp.bfloat16)
+        if c:
+            arrive(c - 1).start()
     gain_a = ga_ref[...].astype(jnp.float32).reshape(1, dim)
     gain_m = gm_ref[...].astype(jnp.float32).reshape(1, dim)
     first, last = span_ref[0], span_ref[1]
@@ -91,6 +112,8 @@
         cos_s[rows, :] = jnp.cos(angle)
         sin_s[rows, :] = jnp.sin(angle) * sign
         start_s[rows, :] = 128 * t + tile_row - pos.astype(jnp.int32)
+        if t == 0:
+            arrive(n_blk - 1).start()
     for c in loads[:4]:
         c.wait()
 
@@ -132,9 +155,9 @@
     def _block(c):
         rows = rows_at(c)
         arrive(c).wait_recv()
-        where_row = c * QB + lax.broadcasted_iota(jnp.int32, (QB, dim), 0)
-        arrived = (where_row >= first) & (where_row < last)
-        r = jnp.where(arrived, rbuf[rows, :].astype(jnp.float32), rloc_ref[rows, :].astype(jnp.float32))
+        trade(c, loc_b, lb, lbs, lbr).wait_recv()
+        fetch(c, loc_a, la, las).wait()
+        r = select(c, first, last, rbuf[rows, :], select(c, span_ref[4], span_ref[5], la[rows, :], lb[rows, :]))
         r_s[...] = r
         h = norm_rows(r, gain_a)
         cos_t = cos_s[rows, :]
@@ -184,13 +207,15 @@
         relay(c)
     for c in range(n_blk):
         arrive(c).wait_send()
+        trade(c, out_b, ob, obs, obr).wait_send()
+        trade(c, loc_b, lb, lbs, lbr).wait_send()
         to_sib(c).wait()
         to_peer(c).wait_send()
         forward(c).wait()
 
 
-def layer(span, outgo, rloc, positions, g_attn, w_q, w_k, w_v, w_o, g_mlp, w_gate, w_up, w_down):
-    n_rows, dim = rloc.shape
+def layer(span, sends, positions, g_attn, w_q, w_k, w_v, w_o, g_mlp, w_gate, w_up, w_down):
+    n_rows, dim = sends[0].shape
     head_dim = w_q.shape[2]
     half_dim = head_dim // 2
     exponent = -2.0 * np.arange(half_dim, dtype=np.float32) / np.float32(head_dim)
@@ -208,19 +233,19 @@
     return pl.pallas_call(
         layer_kernel,
         out_shape=[rows, rows, jax.ShapeDtypeStruct((2 * n_rows, dim), bf)],
-        in_specs=[SM, ANY] + [VM] * 5 + [ANY] * 7,
+        in_specs=[SM] + [ANY] * 4 + [VM] * 4 + [ANY] * 7,
         out_specs=[ANY] * 3,
         scratch_shapes=[
-            pltpu.VMEM((n_rows, dim), bf), pltpu.VMEM((QB, dim), f32), pltpu.VMEM((dim // 128, QB, 128), bf),
+            *[pltpu.VMEM((n_rows, dim), bf)] * 5, pltpu.VMEM((QB, dim), f32), pltpu.VMEM((dim // 128, QB, 128), bf),
             pltpu.VMEM((2, n_rows, 128), bf), pltpu.VMEM((2, n_rows, 128), bf), pltpu.VMEM((QB, dim), bf),
             pltpu.VMEM((QB, ff), bf), pltpu.VMEM((2, QB, dim), bf)]
             + [pltpu.VMEM((QB, n_rows), f32)] * 3
             + [pltpu.VMEM((n_rows, 128), f32), pltpu.VMEM((n_rows, 128), f32), pltpu.VMEM((n_rows, 128), jnp.int32),
                pltpu.VMEM((dim, dim), bf), pltpu.VMEM((128, dim), bf), pltpu.VMEM((128, dim), bf), pltpu.VMEM((dim, dim), bf),
-               pltpu.VMEM((dim, ff), bf), pltpu.VMEM((dim, ff), bf), pltpu.VMEM((ff, dim), bf), dma((7,))] + [dma((n_blk,))] * 9,
+               pltpu.VMEM((dim, ff), bf), pltpu.VMEM((dim, ff), bf), pltpu.VMEM((ff, dim), bf), dma((7,))] + [dma((n_blk,))] * 15,
         compiler_params=pltpu.CompilerParams(collective_id=1, has_side_effects=True, vmem_limit_bytes=67000000),
         name="layer",
-    )(span, outgo, rloc, positions.reshape(-1, 128), freq, g_attn, g_mlp, wq_t, wk_t, wv_t, wo_t, w_gate, w_up, w_down)
+    )(span, *sends, positions.reshape(-1, 128), freq, g_attn, g_mlp, wq_t, wk_t, wv_t, wo_t, w_gate, w_up, w_down)
 
 
 CHUNK = 128
@@ -320,7 +345,7 @@
 
 
 def rows_out(lo, hi, src3, stage, base, dst, sem):
-    first, last = lo // CHUNK, (hi + CHUNK - 1) // CHUNK
+    first, last = lo // CHUNK, jnp.where(hi > lo, (hi + CHUNK - 1) // CHUNK, 0)
 
     def copy(i):
         rows = pl.multiple_of(i * CHUNK, CHUNK)
@@ -356,39 +381,37 @@
         one(i)
 
 
-def pick_kernel(perm, so, sl, ro, rl, perm_b, so_b, sl_b, ro_b, rl_b, own, sib, outgo, rloc, span, tab, out3, stage, sems, out_sems):
-    cap = rloc.shape[0]
-    n_tok = own.shape[0]
+def pick_kernel(perm, so, sl, ro, rl, sl_b, ro_b, own, out_a, out_b, loc_a, loc_b, span, tab, out3, stage, sems, out_sems):
+    cap = loc_a.shape[0]
     me = lax.axis_index("sp")
     core = lax.rem(me, 2)
     chip = me // 2
     mate = me + 1 - 2 * core
     far = 2 * (1 - chip)
-    load_table([(own, None, None), (sib, None, None)], tab, stage, sems)
+    load_table([(own, None, None)], tab, stage, sems)
     n_in = rl[far] + rl[far + 1]
     span[0] = (1 - chip) * (cap - n_in)
     span[1] = (1 - chip) * (cap - n_in) + n_in
 
-    def run(dst_row, src, table_row, at, n):
-        def one(t):
-            out3[slab(dst_row + t), :] = tab[slab(table_row + src[at + t]), :]
-        move_run(n, one)
-
-    goal = far + core
-    n_out = sl[goal] + sl_b[goal]
-    row = chip * (cap - n_out)
-    run(row + core * sl_b[goal], perm, 0, so[goal], sl[goal])
-    run(row + (1 - core) * sl[goal], perm_b, n_tok, so_b[goal], sl_b[goal])
-    finish_out = rows_out(row, row + n_out, out3, stage, 0, outgo, out_sems.at[0])
-    near = chip * n_in
-    run(ro[me], perm, 0, so[me], sl[me])
-    run(ro[mate], perm_b, n_tok, so_b[me], sl_b[me])
-    finish_loc = rows_out(near, near + cap - n_in, out3, stage, cap, rloc, out_sems.at[1])
-    finish_out()
-    finish_loc()
-
-
-def back_place_kernel(perm, so, sl, ro, rl, perm_b, so_b, sl_b, ro_b, rl_b, own, sib, stream, out, tab, out3, stage, sems, out_sems):
+    def far_row(goal):
+        return chip * (cap - sl[goal] - sl_b[goal]) + core * sl_b[goal]
+
+    span[2] = far_row(far + core)
+    span[3] = far_row(far + core) + sl[far + core]
+    span[4] = ro[me]
+    span[5] = ro[me] + sl[me]
+    ends = []
+    for n, (goal, row, dst) in enumerate([(far + 1 - core, far_row(far + 1 - core), out_b), (far + core, far_row(far + core), out_a),
+                                          (mate, ro_b[me], loc_b), (me, ro[me], loc_a)]):
+        def one(t, goal=goal, row=row):
+            out3[slab(row + t), :] = tab[slab(perm[so[goal] + t]), :]
+        move_run(sl[goal], one)
+        ends.append(rows_out(row, row + sl[goal], out3, stage, n * cap, dst, out_sems.at[n]))
+    for end in ends:
+        end()
+
+
+def back_place_kernel(perm, so, sl, ro, rl, sl_b, ro_b, own, sib, stream, out, tab, out3, stage, sems, out_sems):
     cap = own.shape[0]
     n_tok = out.shape[0]
     me = lax.axis_index("sp")
@@ -416,14 +439,14 @@
     rows_out(0, n_tok, out3, stage, 0, out, out_sems.at[0])()
 
 
-def local_call(body, out_shapes, out_specs, n_any, tab_rows, out_rows, dim, name):
+def local_call(body, out_shapes, out_specs, n_any, tab_rows, out_rows, stage_rows, dim, name):
     return pl.pallas_call(
         body,
         out_shape=out_shapes,
-        in_specs=[SM] * 10 + [ANY] * n_any,
+        in_specs=[SM] * 7 + [ANY] * n_any,
         out_specs=out_specs,
         scratch_shapes=[pltpu.VMEM((tab_rows * PITCH, 128), jnp.float32), pltpu.VMEM((out_rows * PITCH, 128), jnp.float32),
-                        pltpu.VMEM((tab_rows, dim), jnp.bfloat16), pltpu.SemaphoreType.DMA((tab_rows // LOAD,)), pltpu.SemaphoreType.DMA((2,))],
+                        pltpu.VMEM((stage_rows, dim), jnp.bfloat16), pltpu.SemaphoreType.DMA((tab_rows // LOAD,)), pltpu.SemaphoreType.DMA((4,))],
         compiler_params=pltpu.CompilerParams(vmem_limit_bytes=66000000),
         name=name,
     )
@@ -438,12 +461,12 @@
         n_tok, dim = hidden.shape
         cap = recv_doc.shape[0]
         plan = [tok_perm, send_off, send_len, recv_off, recv_len]
-        sib_hidden, *sib_plan = share([hidden] + plan, 0)
+        plan += share([send_len, recv_off], 0)
         rows_bf = jax.ShapeDtypeStruct((cap, dim), hidden.dtype)
-        outs = [rows_bf, rows_bf, jax.ShapeDtypeStruct((2,), jnp.int32)]
-        outgo, rloc, span = local_call(pick_kernel, outs, [ANY, ANY, SM], 2, 2 * n_tok, cap, dim, "pick")(*plan, *sib_plan, hidden, sib_hidden)
-        done, sib_done, returned = layer(span, outgo, rloc, recv_pos, g_attn, w_q, w_k, w_v, w_o, g_mlp, w_gate, w_up, w_down)
+        outs = [rows_bf] * 4 + [jax.ShapeDtypeStruct((6,), jnp.int32)]
+        out_a, out_b, loc_a, loc_b, span = local_call(pick_kernel, outs, [ANY] * 4 + [SM], 1, n_tok, cap, 4 * cap, dim, "pick")(*plan, hidden)
+        done, sib_done, returned = layer(span, (out_a, out_b, loc_a, loc_b), recv_pos, g_attn, w_q, w_k, w_v, w_o, g_mlp, w_gate, w_up, w_down)
         out = jax.ShapeDtypeStruct((n_tok, dim), hidden.dtype)
-        return local_call(back_place_kernel, out, ANY, 3, 4 * cap, n_tok, dim, "back_place")(*plan, *sib_plan, done, sib_done, returned)
+        return local_call(back_place_kernel, out, ANY, 3, 4 * cap, n_tok, 4 * cap, dim, "back_place")(*plan, done, sib_done, returned)
 
     return jax.shard_map(per_device, mesh=mesh, in_specs=(row_spec,) + (vec_spec,) * 7 + (rep_spec,) * 9, out_specs=row_spec, check_vma=False)

time: 162 us -> 156 us (0.963)
  Pallas kernels: 159 us -> 153 us
    pallas_call x1, Pallas kernels: 9.84 us -> 1.97 us  [share(): pl.pallas_call(functools.partial(share_kernel, 4), out_shape=[jax.ShapeDt...]
where the time goes in v2:
time: 156 us; the launch traced here: 154 us
  Pallas kernels  153 us (98%)
    pallas_call x1, Pallas kernels, layer(): pl.pallas_call(layer_kernel, out_shape=[rows, rows, jax.ShapeDtypeStruct(...  128 us
    pallas_call x1, Pallas kernels, per_device(): local_call(back_place_kernel, out, ANY, 3, 4 * cap, n_tok, 4 * cap, dim,...  12.3 us
    pallas_call x1, Pallas kernels, per_device(): local_call(pick_kernel, outs, [ANY] * 4 + [SM], 1, n_tok, cap, 4 * cap, d...  11.1 us

profile of v2, /device:TPU:0, one launch (start us, length us, event | category | flops | bytes accessed | tf_op | source)
XLA Modules:
  0.0 153.6 jit_solution(11266334566917177386)
XLA Ops:
  0.0 2.0 %share.1 = (s32[4]{0:T(128)}, s32[4]{0:T(128)}) custom-call(s32[4]{0:T(128)} %sl.3, s32[4]{0:T(128)} %ro.3), custom_call_target="tpu_custom_call" | custom-call | tf_op jit(solution)/shard_map/share/pallas_call | solution.py:293
  2.0 11.1 %pick.1 = (bf16[1536,896]{1,0:T(8,128)(2,1)}, bf16[1536,896]{1,0:T(8,128)(2,1)}, bf16[1536,896]{1,0:T(8,128)(2,1)}, bf16[1536,896]{1,0:T(8,128)(2,1)}, s32[6]{0:T(128)}) custom-call(s32[3072]{0:T(1024)} %perm.3, s32[4]{0:T(128)} %so.3, s32[4]{0:T(128)} %sl.3, s32[4]{0:T(128)} %ro.3, s32[4]{0:T(128)} %rl.3, s32[4]{0:T(128)} %get-tuple-element.15.sl_b, ...), custom_call_target="tpu_custom_call" | custom-call | tf_op jit(solution)/shard_map/pick/pallas_call | solution.py:467
  13.1 128.1 %layer.1 = (bf16[1536,896]{1,0:T(8,128)(2,1)}, bf16[1536,896]{1,0:T(8,128)(2,1)}, bf16[3072,896]{1,0:T(8,128)(2,1)}) custom-call(s32[6]{0:T(128)} %get-tuple-element.17.span_ref, bf16[1536,896]{1,0:T(8,128)(2,1)} %get-tuple-element.18.out_a, bf16[1536,896]{1,0:T(8,128)(2,1)} %get-tuple-element.19.out_b, bf16[1536,896]{1,0:T(8,128)(2,1)} %get-tuple-element.20.loc_a, ...), custom_call_target="tpu_custom_call" | custom-call | tf_op jit(solution)/shard_map/layer/pallas_call | solution.py:233
  141.1 12.3 %back_place.1 = bf16[3072,896]{1,0:T(8,128)(2,1)} custom-call(s32[3072]{0:T(1024)} %perm.3, s32[4]{0:T(128)} %so.3, s32[4]{0:T(128)} %sl.3, s32[4]{0:T(128)} %ro.3, s32[4]{0:T(128)} %rl.3, s32[4]{0:T(128)} %get-tuple-element.15.sl_b, s32[4]{0:T(128)} %get-tuple-element.16.ro_b, bf16[1536,896]{1,0:T(8,128)(2,1)} %get-tuple-element.22.own, ...), custom_call_target="tpu_custom_call" | custom-call | tf_op jit(solution)/shard_map/back_place/pallas_call | solution.py:470

commit v3 on v2

--- a/solution.py
+++ b/solution.py
@@ -12,6 +12,7 @@
 NORM_EPS = 1e-5
 ROWS = 512
 QB = 256
+END = 128
 FT = 256
 
 
@@ -38,7 +39,8 @@
                  as_, ar, ps, pr, ss, sr, fs, fr, own_sem, oas, obs, obr, las, lbs, lbr):
     n_rows, dim = loc_a.shape
     n_pairs = dim // 128
-    n_blk = n_rows // QB
+    n_blk = (n_rows - 2 * END) // QB + 2
+    final = n_blk - 1
     ff = wg_s.shape[1]
     me = lax.axis_index("sp")
     sib = me + 1 - 2 * lax.rem(me, 2)
@@ -48,7 +50,9 @@
     meet([sib, peer])
 
     def rows_at(c):
-        return pl.ds(pl.multiple_of(c * QB, QB), QB)
+        if isinstance(c, int) and c in (0, final):
+            return pl.ds(0 if c == 0 else n_rows - END, END)
+        return pl.ds(pl.multiple_of(END + (c - 1) * QB, END), QB)
 
     def arrive(c):
         return push(ob.at[rows_at(c)], rbuf.at[rows_at(c)], as_.at[c], ar.at[c], peer)
@@ -60,10 +64,12 @@
         return push(own.at[rows_at(c)], sib_out.at[rows_at(c)], ss.at[c], sr.at[c], sib)
 
     def forward(c):
-        return push(far.at[rows_at(c)], far.at[pl.ds(pl.multiple_of(n_rows + c * QB, QB), QB)], fs.at[c], fr.at[c], sib)
+        rows = rows_at(c)
+        return push(far.at[rows], far.at[pl.ds(pl.multiple_of(n_rows + rows.start, END), rows.size)], fs.at[c], fr.at[c], sib)
 
     def keep(c):
-        return pltpu.make_async_copy(obuf.at[lax.rem(c, 2)], own.at[rows_at(c)], own_sem.at[c])
+        rows = rows_at(c)
+        return pltpu.make_async_copy(obuf.at[lax.rem(c, 2), pl.ds(0, rows.size)], own.at[rows], own_sem.at[c])
 
     def send(c):
         keep(c).wait()
@@ -81,7 +87,8 @@
         return push(src.at[rows_at(c)], dst.at[rows_at(c)], send_sem.at[c], recv_sem.at[c], sib)
 
     def select(c, lo, hi, yes, no):
-        row = c * QB + lax.broadcasted_iota(jnp.int32, (QB, dim), 0)
+        rows = rows_at(c)
+        row = rows.start + lax.broadcasted_iota(jnp.int32, (rows.size, dim), 0)
         return jnp.where((row >= lo) & (row < hi), yes.astype(jnp.float32), no.astype(jnp.float32))
 
     for c in range(n_blk):
@@ -117,27 +124,26 @@
     for c in loads[:4]:
         c.wait()
 
-    lane = lax.broadcasted_iota(jnp.int32, (QB, 128), 1)
-    first_half = lane % 64 < 32
-    low = lane < 64
-
-    def attend(c):
-        length = (c + 1) * QB
-        start = start_s[c * QB:(c + 1) * QB, :]
-        row = c * QB + lax.broadcasted_iota(jnp.int32, (QB, 128), 0)
+    def attend(at, size):
+        length = at + size
+        mine = pl.ds(0, size)
+        lane = lax.broadcasted_iota(jnp.int32, (size, 128), 1)
+        low = lane < 64
+        start = start_s[at:length, :]
+        row = at + lax.broadcasted_iota(jnp.int32, (size, 128), 0)
         for t in range(length // 128):
             col = 128 * t + lane
-            bias[:, 128 * t:128 * (t + 1)] = jnp.where((col >= start) & (col <= row), 3e38, -1e30)
+            bias[mine, 128 * t:128 * (t + 1)] = jnp.where((col >= start) & (col <= row), 3e38, -1e30)
 
         def scores(p, half, dst):
-            qp = q_s[p]
+            qp = q_s[p, mine, :]
             qh = jnp.where(low if half == 0 else ~low, qp, jnp.zeros_like(qp))
-            s = jnp.minimum(dot_t(qh, k_s[(2 * p + half) // 7, :length, :]), bias[:, :length])
-            dst[:, :length] = s
+            s = jnp.minimum(dot_t(qh, k_s[(2 * p + half) // 7, :length, :]), bias[mine, :length])
+            dst[mine, :length] = s
             return jnp.max(s, axis=1, keepdims=True)
 
         def soft(p, half, src, top):
-            e = jnp.exp(src[:, :length] - top)
+            e = jnp.exp(src[mine, :length] - top)
             total = jnp.sum(e, axis=1, keepdims=True)
             return dot_n(e.astype(jnp.bfloat16), v_s[(2 * p + half) // 7, :length, :]) / total
 
@@ -146,26 +152,30 @@
             out_a = soft(p, 0, sa, top_a)
             top_a = scores(jnp.minimum(p + 1, n_pairs - 1), 0, sa)
             out_b = soft(p, 1, sb, top_b)
-            o_s[:, pl.ds(pl.multiple_of(p * 128, 128), 128)] = jnp.where(low, out_a, out_b).astype(jnp.bfloat16)
+            o_s[mine, pl.ds(pl.multiple_of(p * 128, 128), 128)] = jnp.where(low, out_a, out_b).astype(jnp.bfloat16)
             return top_a
 
         lax.fori_loop(0, n_pairs, pair, scores(0, 0, sa))
 
-    @pl.loop(0, n_blk)
-    def _block(c):
+    def block(c, attention, before_mlp):
         rows = rows_at(c)
-        arrive(c).wait_recv()
+        size = rows.size
+        mine = pl.ds(0, size)
+        lane = lax.broadcasted_iota(jnp.int32, (size, 128), 1)
+        first_half = lane % 64 < 32
+        low = lane < 64
         trade(c, loc_b, lb, lbs, lbr).wait_recv()
         fetch(c, loc_a, la, las).wait()
+        arrive(c).wait_recv()
         r = select(c, first, last, rbuf[rows, :], select(c, span_ref[4], span_ref[5], la[rows, :], lb[rows, :]))
-        r_s[...] = r
+        r_s[mine, :] = r
         h = norm_rows(r, gain_a)
         cos_t = cos_s[rows, :]
         sin_t = sin_s[rows, :]
         q = dot_t(h, wq_s[...])
         for p in range(n_pairs):
             qp = rope_pair(q[:, 128 * p:128 * (p + 1)], cos_t, sin_t, first_half)
-            q_s[p] = (qp.astype(jnp.bfloat16) * 0.125).astype(jnp.bfloat16)
+            q_s[p, mine, :] = (qp.astype(jnp.bfloat16) * 0.125).astype(jnp.bfloat16)
         k = rope_pair(dot_t(h, wk_s[...]), cos_t, sin_t, first_half)
         v = dot_t(h, wv_s[...])
         for s, x in ((k_s, k), (v_s, v)):
@@ -173,37 +183,53 @@
             s[0, rows, :] = jnp.where(low, x, other).astype(jnp.bfloat16)
             s[1, rows, :] = jnp.where(low, other, x).astype(jnp.bfloat16)
 
-        for at in range(n_blk):
-            pl.when(c == at)(functools.partial(attend, at))
-
-        @pl.when(c >= 1)
-        def _send():
-            send(c - 1)
-
-        @pl.when(c >= 4)
-        def _relay():
-            relay(c - 4)
-
-        @pl.when(c == 0)
-        def _weights():
-            for x in loads[4:]:
-                x.wait()
-
-        attn = dot_n(o_s[...], wo_s[...]).astype(jnp.bfloat16)
-        z = (r_s[...] + attn.astype(jnp.float32)).astype(jnp.bfloat16).astype(jnp.float32)
-        r_s[...] = z
+        attention()
+        before_mlp()
+        attn = dot_n(o_s[mine, :], wo_s[...]).astype(jnp.bfloat16)
+        z = (r_s[mine, :] + attn.astype(jnp.float32)).astype(jnp.bfloat16).astype(jnp.float32)
+        r_s[mine, :] = z
         h = norm_rows(z, gain_m)
         for t in range(ff // FT):
             cols = slice(t * FT, (t + 1) * FT)
             gate = 0.5 * dot_n(h, wg_s[:, cols])
             up = dot_n(h, wu_s[:, cols])
-            m_s[:, cols] = ((gate + gate * jnp.tanh(gate)) * up).astype(jnp.bfloat16)
-        down = dot_n(m_s[...], wd_s[...]).astype(jnp.bfloat16)
-        obuf[lax.rem(c, 2)] = (r_s[...] + down.astype(jnp.float32)).astype(jnp.bfloat16)
+            m_s[mine, cols] = ((gate + gate * jnp.tanh(gate)) * up).astype(jnp.bfloat16)
+        down = dot_n(m_s[mine, :], wd_s[...]).astype(jnp.bfloat16)
+        obuf[lax.rem(c, 2), mine, :] = (r_s[mine, :] + down.astype(jnp.float32)).astype(jnp.bfloat16)
         keep(c).start()
 
-    send(n_blk - 1)
-    for c in range(n_blk - 4, n_blk):
+    def weights():
+        for x in loads[4:]:
+            x.wait()
+
+    def send_before(c):
+        @pl.when(c == 1)
+        def _first():
+            send(0)
+
+        @pl.when(c > 1)
+        def _other():
+            send(c - 1)
+
+    def ending():
+        send(final - 1)
+        relay(0)
+        relay(1)
+        relay(2)
+
+    block(0, lambda: attend(0, END), weights)
+
+    @pl.loop(1, final)
+    def _block(c):
+        def attention():
+            for at in range(1, final):
+                pl.when(c == at)(functools.partial(attend, END + (at - 1) * QB, QB))
+
+        block(c, attention, lambda: send_before(c))
+
+    block(final, lambda: attend(n_rows - END, END), ending)
+    send(final)
+    for c in range(3, n_blk):
         relay(c)
     for c in range(n_blk):
         arrive(c).wait_send()
@@ -226,7 +252,7 @@
     wv_t = jnp.transpose(w_v, (1, 2, 0)).reshape(128, dim)
     wo_t = w_o.reshape(dim, dim)
     bf, f32 = jnp.bfloat16, jnp.float32
-    n_blk = n_rows // QB
+    n_blk = (n_rows - 2 * END) // QB + 2
     ff = w_gate.shape[1]
     rows = jax.ShapeDtypeStruct((n_rows, dim), bf)
     dma = pltpu.SemaphoreType.DMA

time: 156 us -> 155 us (level)
    pallas_call x1, Pallas kernels: 128 us -> 134 us  [layer(): pl.pallas_call(layer_kernel, out_shape=[rows, rows, jax.ShapeDtypeStruct(...]
    pallas_call x1, Pallas kernels: 11.1 us -> 7.18 us  [per_device(): local_call(pick_kernel, outs, [ANY] * 4 + [SM], 1, n_tok, cap, 4 * cap, d...]
where the time goes in v3:
time: 155 us; the launch traced here: 154 us
  Pallas kernels  154 us (99%)
    pallas_call x1, Pallas kernels, layer(): pl.pallas_call(layer_kernel, out_shape=[rows, rows, jax.ShapeDtypeStruct(...  134 us
    pallas_call x1, Pallas kernels, per_device(): local_call(back_place_kernel, out, ANY, 3, 4 * cap, n_tok, 4 * cap, dim,...  10.7 us
    pallas_call x1, Pallas kernels, per_device(): local_call(pick_kernel, outs, [ANY] * 4 + [SM], 1, n_tok, cap, 4 * cap, d...  7.18 us

profile of v3, /device:TPU:0, one launch (start us, length us, event | category | flops | bytes accessed | tf_op | source)
XLA Modules:
  0.0 154.0 jit_solution(11976493278816899833)
XLA Ops:
  0.0 2.0 %share.1 = (s32[4]{0:T(128)}, s32[4]{0:T(128)}) custom-call(s32[4]{0:T(128)} %sl.3, s32[4]{0:T(128)} %ro.3), custom_call_target="tpu_custom_call" | custom-call | tf_op jit(solution)/shard_map/share/pallas_call | solution.py:319
  2.0 7.2 %pick.1 = (bf16[1536,896]{1,0:T(8,128)(2,1)}, bf16[1536,896]{1,0:T(8,128)(2,1)}, bf16[1536,896]{1,0:T(8,128)(2,1)}, bf16[1536,896]{1,0:T(8,128)(2,1)}, s32[6]{0:T(128)}) custom-call(s32[3072]{0:T(1024)} %perm.3, s32[4]{0:T(128)} %so.3, s32[4]{0:T(128)} %sl.3, s32[4]{0:T(128)} %ro.3, s32[4]{0:T(128)} %rl.3, s32[4]{0:T(128)} %get-tuple-element.15.sl_b, ...), custom_call_target="tpu_custom_call" | custom-call | tf_op jit(solution)/shard_map/pick/pallas_call | solution.py:493
  9.2 133.9 %layer.1 = (bf16[1536,896]{1,0:T(8,128)(2,1)}, bf16[1536,896]{1,0:T(8,128)(2,1)}, bf16[3072,896]{1,0:T(8,128)(2,1)}) custom-call(s32[6]{0:T(128)} %get-tuple-element.17.span_ref, bf16[1536,896]{1,0:T(8,128)(2,1)} %get-tuple-element.18.out_a, bf16[1536,896]{1,0:T(8,128)(2,1)} %get-tuple-element.19.out_b, bf16[1536,896]{1,0:T(8,128)(2,1)} %get-tuple-element.20.loc_a, ...), custom_call_target="tpu_custom_call" | custom-call | tf_op jit(solution)/shard_map/layer/pallas_call | solution.py:259
  143.1 10.7 %back_place.1 = bf16[3072,896]{1,0:T(8,128)(2,1)} custom-call(s32[3072]{0:T(1024)} %perm.3, s32[4]{0:T(128)} %so.3, s32[4]{0:T(128)} %sl.3, s32[4]{0:T(128)} %ro.3, s32[4]{0:T(128)} %rl.3, s32[4]{0:T(128)} %get-tuple-element.15.sl_b, s32[4]{0:T(128)} %get-tuple-element.16.ro_b, bf16[1536,896]{1,0:T(8,128)(2,1)} %get-tuple-element.22.own, ...), custom_call_target="tpu_custom_call" | custom-call | tf_op jit(solution)/shard_map/back_place/pallas_call | solution.py:496
